TPU v7x, 256 devices: a 8x8x2 block of a 8x8x16 slice. The times are simulated.
256 devices in a mesh: layout: 2 (over z), tile: 64 (over x, y), chan: 2 (over core).
Axes of the slice: x: 8, y: 8, z: 2, core: 2. Of those that a mesh axis runs over, the one named last changes fastest.
The devices are a block of a 8x8x16 slice.
Arguments:
- sample_weight: float32 [256, 64, 256], P(('layout', 'tile', 'chan')), parts along dimension 0, may hold values from 0.25 to 4
- fraction_u: float32 [256, 64, 256], P(('layout', 'tile', 'chan')), parts along dimension 0, may hold values from 0 to 1
- fraction_v: float32 [256, 64, 256], P(('layout', 'tile', 'chan')), parts along dimension 0, may hold values from 0 to 1
- cell_code: int32 [256, 64, 256], P(('layout', 'tile', 'chan')), parts along dimension 0, may hold values from 260 to 3835, as said below
- tile_fill: int32 [256, 64, 64], P(('layout', 'tile', 'chan')), parts along dimension 0, may hold values from 0 to 4, as said below
Outputs:
- psf: float32 [8192, 4096], P(('layout', 'tile', 'chan')), parts along dimension 0
There are 2 independent parts, one for each index of `layout`. A program takes and returns all parts, laid end to end along the dimension named above; each array names one. Nothing has to cross between parts.
Inputs may be any that keep to these rules, and one draw needn't show every extreme that they name: `cell_code`: row offset and column offset each lie in 4 .. 59. `tile_fill`: some uv tile is full from every sender; tiles near the grid's centre hold more samples than outer ones.
All inputs are finite; a program needn't handle non-finite values.
Results may differ from a plain program's by a relative error of at most 0.0003.
Values sent between devices are 32-bit elements; how exact they have to be, the bound alone decides.
A program may use at most 64 MiB of HBM per device.

v0:
```python
import functools
import math

import jax
import jax.numpy as jnp
import numpy as np
from jax import lax
from jax.experimental import pallas as pl
from jax.experimental.pallas import tpu as pltpu
from jax.sharding import PartitionSpec as P

G = 4096
TILE = 64
CAP = 4
NT = 64
LANES = 128
QUARTERS = 4
ROWS = TILE // QUARTERS
BLOCKS = G // LANES
OUT_ROWS = 32
MESH = pl.DeviceIdType.MESH
F32 = jnp.float32
BF16 = jnp.bfloat16


def two_parts(table):
    table = np.asarray(table, np.float32)
    high = table.astype(BF16)
    low = (table - high.astype(np.float32)).astype(BF16)
    return np.concatenate([high, low], axis=0)


@functools.lru_cache
def tables(devices):
    spread = (np.arange(NT)[:, None] == np.arange(NT * CAP)[None, :] // CAP).astype(BF16)
    turn = 2.0 * np.pi * np.outer(np.arange(LANES), np.arange(LANES)) / LANES
    cos, sin = np.cos(turn), np.sin(turn)
    row_table = two_parts(np.block([[cos, -sin], [sin, cos]]))
    turn = 2.0 * np.pi * np.outer(np.arange(BLOCKS), np.arange(LANES)) / G
    row_twist = np.stack([np.cos(turn), np.sin(turn)]).astype(np.float32)
    wide = G // ROWS
    turn = 2.0 * np.pi * np.outer(np.arange(wide), np.arange(devices)) / wide
    cos, sin = np.cos(turn), np.sin(turn)
    col_table = two_parts(np.block([[cos, -sin], [sin, cos]]))
    turn = 2.0 * np.pi * np.outer(np.arange(wide), np.arange(LANES) % ROWS) / G
    col_twist = np.stack([np.cos(turn), np.sin(turn)]).astype(np.float32)
    group = LANES // ROWS
    out_index = np.arange(ROWS * group)
    lane = np.arange(LANES)
    same = (out_index[:, None] % group == lane[None, :] // ROWS) / math.sqrt(devices * NT * NT * CAP)
    turn = 2.0 * np.pi * np.outer(out_index // group, lane % ROWS) / ROWS
    last_table = two_parts(np.concatenate([same * np.cos(turn), -same * np.sin(turn)], axis=1))
    return spread, row_table, row_twist, col_table, col_twist, last_table


def split(value):
    high = value.astype(BF16)
    return high, (value - high.astype(F32)).astype(BF16)


def dot(left, right, right_dim):
    return lax.dot_general(left, right, (((1,), (right_dim,)), ((), ())), preferred_element_type=F32)


def table_dot(table, value, right_dim):
    high, low = split(value)
    half = table.shape[0] // 2
    both = dot(table[...], high, right_dim)
    return both[:half] + both[half:] + dot(table[:half], low, right_dim)


def times(value, real, imag):
    v_re, v_im = value
    if abs(imag) < 1e-12:
        if abs(real - 1.0) < 1e-12:
            return value
        return v_re * real, None if v_im is None else v_im * real
    if v_im is None:
        return (None if abs(real) < 1e-12 else v_re * real), v_re * imag
    if abs(real) < 1e-12:
        return -v_im * imag, v_re * imag
    return v_re * real - v_im * imag, v_re * imag + v_im * real


def plus(a, b, sign):
    if b is None:
        return a
    if a is None:
        return b if sign > 0 else -b
    return a + b if sign > 0 else a - b


def real_transform(values):
    count = len(values)
    if count == 1:
        return [(values[0], None)]
    if count == 2:
        return [(values[0] + values[1], None), (values[0] - values[1], None)]
    even, odd = real_transform(values[0::2]), real_transform(values[1::2])
    out = [None] * (count // 2 + 1)
    for k in range(count // 4 + 1):
        turn = 2.0 * math.pi * k / count
        turned = times(odd[k], math.cos(turn), math.sin(turn))
        out[k] = (plus(even[k][0], turned[0], 1), plus(even[k][1], turned[1], 1))
        far_im = plus(even[k][1], turned[1], -1)
        out[count // 2 - k] = (plus(even[k][0], turned[0], -1), None if far_im is None else -far_im)
    return out


def kernel(
    tiles,
    chans,
    weight,
    frac_u,
    frac_v,
    code,
    fill,
    spread,
    row_table,
    row_twist,
    col_table,
    col_twist,
    last_table,
    out,
    sample,
    packed,
    landed,
    sorted_,
    slab,
    rows,
    high,
    low,
    spectrum,
    columns,
    send_a,
    recv_a,
    send_x,
    recv_x,
    send_b,
    recv_b,
):
    count = tiles * chans
    layout = lax.axis_index("layout")
    me = lax.axis_index("tile") * chans + lax.axis_index("chan")
    mine = lax.rem(me, QUARTERS)

    def place(index):
        return (layout, lax.div(index, chans), lax.rem(index, chans))

    def peer(step):
        return lax.rem(me + step, count)

    def await_bytes(ref, sem):
        pltpu.make_async_copy(ref, ref, sem).wait()

    barrier = pltpu.get_barrier_semaphore()

    @pl.loop(1, count)
    def _(step):
        pl.semaphore_signal(barrier, inc=1, device_id=place(peer(step)), device_id_type=MESH)

    fill_wide = dot(fill[0].astype(F32).astype(BF16), spread[...], 0)
    slot = lax.broadcasted_iota(jnp.int32, (NT, NT * CAP), 1) % CAP
    sample[0] = jnp.where(slot.astype(F32) < fill_wide, weight[0], 0.0)
    far = lax.broadcasted_iota(jnp.int32, (NT, NT * CAP), 0) >= NT // 2
    for part, position in (
        (1, (code[0] >> 6).astype(F32) + frac_u[0]),
        (2, (code[0] & (TILE - 1)).astype(F32) + frac_v[0]),
    ):
        sample[part] = jnp.where(far, TILE - position, position) * 0.25

    lower = lax.broadcasted_iota(jnp.int32, (1, LANES), 1) < LANES // 2

    @pl.loop(0, NT // 2)
    def _(p):
        for part in range(3):
            near = sample[part, pl.ds(p, 1), :]
            away = sample[part, pl.ds(NT - 1 - p, 1), :]
            for q in range(QUARTERS):
                a = near[:, (q // 2) * LANES : (q // 2 + 1) * LANES]
                b = away[:, (1 - q // 2) * LANES : (2 - q // 2) * LANES]
                if q % 2 == 0:
                    row = jnp.where(lower, a, b)
                else:
                    row = pltpu.roll(jnp.where(lower, b, a), LANES // 2, 1)
                packed[QUARTERS * p + q, pl.ds(part, 1), :] = row

    pl.semaphore_wait(barrier, count - 1)

    @pl.loop(1, count)
    def _(step):
        to = peer(step)
        pltpu.make_async_remote_copy(
            src_ref=packed.at[to],
            dst_ref=landed.at[me],
            send_sem=send_a,
            recv_sem=recv_a,
            device_id=place(to),
            device_id_type=MESH,
        ).start()

    landed[me] = packed[me]
    await_bytes(landed.at[pl.ds(0, count - 1)], recv_a)

    for part in range(3):
        sorted_[part] = landed[:, part, :].T

    cell = lax.broadcasted_iota(jnp.int32, (TILE, count), 0).astype(F32) * 0.25

    def taper(row, where):
        scaled = cell - row[where]
        inner = jnp.maximum(1.0 - scaled * scaled, 0.0)
        return inner * inner

    def one_tile(k):
        total = jnp.zeros((2 * TILE, 2 * TILE), F32)
        starts = [CAP * k, NT * CAP // 2 - CAP - CAP * k]
        for start in starts:
            for pair in range(CAP // 2):
                lefts, rights = [], []
                for slot in range(2):
                    where = pl.ds(start + 2 * pair + slot, 1)
                    u_high, u_low = split(taper(sorted_.at[1], where) * sorted_[0, where])
                    v_high, v_low = split(taper(sorted_.at[2], where))
                    lefts.append(jnp.concatenate([u_high, u_low], axis=0))
                    rights.append(jnp.concatenate([v_high, v_low], axis=0))
                total += dot(jnp.concatenate(lefts, axis=1), jnp.concatenate(rights, axis=1), 1)
        return total[:TILE] + total[TILE:]

    upper_half = lax.broadcasted_iota(jnp.int32, (TILE, LANES), 1) >= TILE

    @pl.loop(0, NT // QUARTERS // 2)
    def _(pair):
        first, second = one_tile(2 * pair), one_tile(2 * pair + 1)
        first = first + pltpu.roll(first, TILE, 1)
        second = second + pltpu.roll(second, TILE, 1)
        slab[pair] = jnp.where(upper_half, second, first)

    strip = BLOCKS // QUARTERS
    for hop in range(1, QUARTERS):
        other = lax.rem(mine + hop, QUARTERS)
        pltpu.make_async_remote_copy(
            src_ref=slab.at[:, pl.ds(pl.multiple_of(other * ROWS, ROWS), ROWS), :],
            dst_ref=rows.at[pl.ds(mine * strip, strip)],
            send_sem=send_x,
            recv_sem=recv_x,
            device_id=place(me - mine + other),
            device_id_type=MESH,
        ).start()
    rows[pl.ds(mine * strip, strip)] = slab[:, pl.ds(pl.multiple_of(mine * ROWS, ROWS), ROWS), :]
    await_bytes(rows.at[pl.ds(0, BLOCKS - strip)], recv_x)

    waves = real_transform([rows[t] for t in range(BLOCKS)])
    for k in range(BLOCKS):
        re, im = waves[min(k, BLOCKS - k)]
        c, s = row_twist[0, k : k + 1, :], row_twist[1, k : k + 1, :]
        if im is None:
            turned = (re * c, re * s)
        elif k <= BLOCKS // 2:
            turned = (re * c - im * s, re * s + im * c)
        else:
            turned = (re * c + im * s, re * s - im * c)
        for part in range(2):
            upper, rest = split(turned[part])
            high[ROWS * k : ROWS * (k + 1), LANES * part : LANES * (part + 1)] = upper
            low[ROWS * k : ROWS * (k + 1), LANES * part : LANES * (part + 1)] = rest
    groups = BLOCKS * ROWS // LANES
    for lane in range(0, groups, 2):
        where = slice(LANES * lane, LANES * (lane + 2))
        both = dot(row_table[...], high[where], 1)
        half = 2 * LANES
        both = both[:half] + both[half:] + dot(row_table[:half], low[where], 1)
        for part in range(2):
            for extra in range(2):
                spectrum[pl.ds(part * groups + lane + extra, count, stride=2 * groups), :] = both[
                    part * LANES : (part + 1) * LANES, extra * LANES : (extra + 1) * LANES
                ]

    each = 2 * groups

    def block(ref, index):
        return ref.at[pl.ds(pl.multiple_of(index * each, each), each), :]

    @pl.loop(1, count)
    def _(step):
        to = peer(step)
        pltpu.make_async_remote_copy(
            src_ref=block(spectrum, to),
            dst_ref=block(columns, me),
            send_sem=send_b,
            recv_sem=recv_b,
            device_id=place(to),
            device_id_type=MESH,
        ).start()

    own = pl.ds(pl.multiple_of(me * each, each), each)
    columns[own, :] = spectrum[own, :]
    await_bytes(columns.at[pl.ds(0, (count - 1) * each), :], recv_b)

    wide = G // ROWS
    for lane in range(groups):
        real = columns[pl.ds(lane, count, stride=each), :]
        imag = columns[pl.ds(groups + lane, count, stride=each), :]
        first = table_dot(col_table, jnp.concatenate([real, imag], axis=0), 0)
        re, im = first[:wide], first[wide:]
        c, s = col_twist[0], col_twist[1]
        turned = jnp.concatenate([re * c - im * s, re * s + im * c], axis=1)
        last = table_dot(last_table, turned, 1)
        tall = LANES // ROWS
        for l2 in range(ROWS):
            out[tall * lane : tall * (lane + 1), wide * l2 : wide * (l2 + 1)] = last[tall * l2 : tall * (l2 + 1)]

    await_bytes(packed.at[pl.ds(0, count - 1)], send_a)
    await_bytes(rows.at[pl.ds(0, BLOCKS - strip)], send_x)
    await_bytes(columns.at[pl.ds(0, (count - 1) * each), :], send_b)


def body(sample_weight, fraction_u, fraction_v, cell_code, tile_fill):
    tiles, chans = lax.axis_size("tile"), lax.axis_size("chan")
    count = tiles * chans
    constants = [jnp.asarray(table) for table in tables(count)]
    return pl.pallas_call(
        functools.partial(kernel, tiles, chans),
        out_shape=jax.ShapeDtypeStruct((OUT_ROWS, G), F32),
        in_specs=[pl.BlockSpec(memory_space=pltpu.VMEM)] * (5 + len(constants)),
        out_specs=pl.BlockSpec(memory_space=pltpu.VMEM),
        scratch_shapes=[
            pltpu.VMEM((3, NT, NT * CAP), F32),
            pltpu.VMEM((count, 3, LANES), F32),
            pltpu.VMEM((count, 3, LANES), F32),
            pltpu.VMEM((3, LANES, count), F32),
            pltpu.VMEM((BLOCKS // QUARTERS, TILE, LANES), F32),
            pltpu.VMEM((BLOCKS, ROWS, LANES), F32),
            pltpu.VMEM((BLOCKS * ROWS, 2 * LANES), BF16),
            pltpu.VMEM((BLOCKS * ROWS, 2 * LANES), BF16),
            pltpu.VMEM((count * 8, LANES), F32),
            pltpu.VMEM((count * 8, LANES), F32),
        ]
        + [pltpu.SemaphoreType.DMA] * 6,
        compiler_params=pltpu.CompilerParams(collective_id=0, has_side_effects=True),
    )(sample_weight, fraction_u, fraction_v, cell_code, tile_fill, *constants)


def solution(mesh):
    spec = P(("layout", "tile", "chan"), None, None)
    return jax.shard_map(
        body,
        mesh=mesh,
        in_specs=(spec,) * 5,
        out_specs=P(("layout", "tile", "chan"), None),
        check_vma=False,
    )
```

profile of v0, /device:TPU:513, one launch (start us, length us, event | category | flops | bytes accessed | tf_op | source)
XLA Modules:
  0.0 68.7 jit_solution(2171594856730194933)
XLA Ops:
  0.0 66.8 %shard_map.109 = f32[32,4096]{1,0:T(8,128)} custom-call(f32[1,64,256]{2,1,0:T(8,128)} %weight.1, f32[1,64,256]{2,1,0:T(8,128)} %frac_u.1, f32[1,64,256]{2,1,0:T(8,128)} %frac_v.1, s32[1,64,256]{2,1,0:T(8,128)} %code.1, s32[1,64,64]{2,1,0:T(8,128)} %fill.1, bf16[64,256]{1,0:T(8,128)(2,1)} %constant.12.clone.spread, ...), custom_call_target="tpu_custom_call" | custom-call | tf_op jit(solution)/shard_map/pallas_call | solution.py:322
  66.8 1.9 %copy.13 = f32[32,4096]{1,0:T(8,128)} copy(f32[32,4096]{1,0:T(8,128)} %shard_map.109) | data formatting | bytes 1048576
where the time goes:
time: 68.9 us; the launch traced here: 68.7 us
  Pallas kernels  66.8 us (97%)
  local copies, waits for them, and re-layouts  1.87 us (3%)
    pallas_call x1, Pallas kernels, body(): pl.pallas_call(functools.partial(kernel, tiles, chans), out_shape=jax.Sha...  66.8 us
    unnamed x1, local copies, waits for them, and re-layouts  1.87 us

commit v1 on v0

--- a/solution.py
+++ b/solution.py
@@ -107,57 +107,65 @@
     return out
 
 
-def kernel(
-    tiles,
-    chans,
-    weight,
-    frac_u,
-    frac_v,
-    code,
-    fill,
-    spread,
-    row_table,
-    row_twist,
-    col_table,
-    col_twist,
-    last_table,
-    out,
-    sample,
-    packed,
-    landed,
-    sorted_,
-    slab,
-    rows,
-    high,
-    low,
-    spectrum,
-    columns,
-    send_a,
-    recv_a,
-    send_x,
-    recv_x,
-    send_b,
-    recv_b,
-):
+def kernel(tiles, chans, *refs):
+    inputs, tables_in, refs = refs[:5], refs[5:11], refs[11:]
+    out, refs = refs[0], refs[1:]
+    weight, frac_u, frac_v, code, fill = refs[:5]
+    spread, row_table, row_twist, col_table, col_twist, last_table = refs[5:11]
+    sample, packed, middle, landed, sorted_, slab, rows, high, low, spectrum, columns = refs[11:22]
+    load, send_1, recv_1, send_2, recv_2, send_x, recv_x, send_b, recv_b = refs[22:]
+    side = math.isqrt(tiles)
     count = tiles * chans
-    layout = lax.axis_index("layout")
-    me = lax.axis_index("tile") * chans + lax.axis_index("chan")
+    line = side * chans
+    layout, tile, chan = lax.axis_index("layout"), lax.axis_index("tile"), lax.axis_index("chan")
+    x, y = lax.div(tile, side), lax.rem(tile, side)
+    in_line = x * chans + chan
+    me = tile * chans + chan
     mine = lax.rem(me, QUARTERS)
-
-    def place(index):
-        return (layout, lax.div(index, chans), lax.rem(index, chans))
-
-    def peer(step):
-        return lax.rem(me + step, count)
+    far_first = sorted(range(side), key=lambda d: -min(d, side - d))
+
+    def ahead(value, step):
+        value = value + step
+        return jnp.where(value >= side, value - side, value)
+
+    def behind(value, step):
+        value = value - step
+        return jnp.where(value < 0, value + side, value)
+
+    def place(to_x, to_y, to_chan):
+        return (layout, to_x * side + to_y, to_chan)
+
+    def send(src, dst, send_sem, recv_sem, device):
+        pltpu.make_async_remote_copy(
+            src_ref=src,
+            dst_ref=dst,
+            send_sem=send_sem,
+            recv_sem=recv_sem,
+            device_id=device,
+            device_id_type=MESH,
+        ).start()
 
     def await_bytes(ref, sem):
         pltpu.make_async_copy(ref, ref, sem).wait()
 
+    line_peers = [
+        (ahead(x, dx), chan if e == 0 else 1 - chan) for dx in far_first for e in range(chans) if (dx, e) != (0, 0)
+    ]
+    column_peers = [ahead(y, dy) for dy in far_first if dy != 0]
     barrier = pltpu.get_barrier_semaphore()
-
-    @pl.loop(1, count)
-    def _(step):
-        pl.semaphore_signal(barrier, inc=1, device_id=place(peer(step)), device_id_type=MESH)
+    for to_x, to_chan in line_peers:
+        pl.semaphore_signal(barrier, inc=1, device_id=place(to_x, y, to_chan), device_id_type=MESH)
+    for to_y in column_peers:
+        pl.semaphore_signal(barrier, inc=1, device_id=place(x, to_y, chan), device_id_type=MESH)
+
+    loads = [
+        pltpu.make_async_copy(src, dst, load.at[k])
+        for k, (src, dst) in enumerate(zip([*inputs, *tables_in], refs[:11], strict=True))
+    ]
+    for k in (4, 5, 0, 3, 1, 2, 6, 7, 8, 9, 10):
+        loads[k].start()
+    for k in range(6):
+        loads[k].wait()
 
     fill_wide = dot(fill[0].astype(F32).astype(BF16), spread[...], 0)
     slot = lax.broadcasted_iota(jnp.int32, (NT, NT * CAP), 1) % CAP
@@ -171,39 +179,42 @@
 
     lower = lax.broadcasted_iota(jnp.int32, (1, LANES), 1) < LANES // 2
 
-    @pl.loop(0, NT // 2)
-    def _(p):
-        for part in range(3):
-            near = sample[part, pl.ds(p, 1), :]
-            away = sample[part, pl.ds(NT - 1 - p, 1), :]
-            for q in range(QUARTERS):
-                a = near[:, (q // 2) * LANES : (q // 2 + 1) * LANES]
-                b = away[:, (1 - q // 2) * LANES : (2 - q // 2) * LANES]
-                if q % 2 == 0:
-                    row = jnp.where(lower, a, b)
-                else:
-                    row = pltpu.roll(jnp.where(lower, b, a), LANES // 2, 1)
-                packed[QUARTERS * p + q, pl.ds(part, 1), :] = row
-
-    pl.semaphore_wait(barrier, count - 1)
-
-    @pl.loop(1, count)
-    def _(step):
-        to = peer(step)
-        pltpu.make_async_remote_copy(
-            src_ref=packed.at[to],
-            dst_ref=landed.at[me],
-            send_sem=send_a,
-            recv_sem=recv_a,
-            device_id=place(to),
-            device_id_type=MESH,
-        ).start()
-
-    landed[me] = packed[me]
-    await_bytes(landed.at[pl.ds(0, count - 1)], recv_a)
+    @pl.loop(0, side)
+    def _(to_x):
+        for near_y in range(side // 2):
+            p = to_x * (side // 2) + near_y
+            for part in range(3):
+                near = sample[part, pl.ds(p, 1), :]
+                away = sample[part, pl.ds(NT - 1 - p, 1), :]
+                for q in range(QUARTERS):
+                    a = near[:, (q // 2) * LANES : (q // 2 + 1) * LANES]
+                    b = away[:, (1 - q // 2) * LANES : (2 - q // 2) * LANES]
+                    if q % 2 == 0:
+                        row = jnp.where(lower, a, b)
+                    else:
+                        row = pltpu.roll(jnp.where(lower, b, a), LANES // 2, 1)
+                    to_y, to_chan = 2 * near_y + q // 2, q % 2
+                    packed[(to_x * chans + to_chan) * side + to_y, pl.ds(part, 1), :] = row
+
+    pl.semaphore_wait(barrier, len(line_peers) + len(column_peers))
+
+    for to_x, to_chan in line_peers:
+        send(
+            packed.at[pl.ds((to_x * chans + to_chan) * side, side)],
+            middle.at[:, in_line],
+            send_1,
+            recv_1,
+            place(to_x, y, to_chan),
+        )
+    middle[:, in_line] = packed[pl.ds(in_line * side, side)]
+    await_bytes(packed.at[pl.ds(0, (line - 1) * side)], recv_1)
+    for to_y in column_peers:
+        send(middle.at[to_y], landed.at[y], send_2, recv_2, place(x, to_y, chan))
+    landed[y] = middle[y]
+    await_bytes(landed.at[pl.ds(0, side - 1)], recv_2)
 
     for part in range(3):
-        sorted_[part] = landed[:, part, :].T
+        sorted_[part] = landed[:, :, part, :].reshape(count, LANES).T
 
     cell = lax.broadcasted_iota(jnp.int32, (TILE, count), 0).astype(F32) * 0.25
 
@@ -228,26 +239,28 @@
         return total[:TILE] + total[TILE:]
 
     upper_half = lax.broadcasted_iota(jnp.int32, (TILE, LANES), 1) >= TILE
-
-    @pl.loop(0, NT // QUARTERS // 2)
+    strip = BLOCKS // QUARTERS
+    others = []
+    for hop in range(1, QUARTERS):
+        other = lax.rem(mine + hop, QUARTERS)
+        index = me - mine + other
+        others.append((other, (layout, lax.div(index, chans), lax.rem(index, chans))))
+
+    def row_range(index):
+        return pl.ds(pl.multiple_of(index * ROWS, ROWS), ROWS)
+
+    @pl.loop(0, strip)
     def _(pair):
         first, second = one_tile(2 * pair), one_tile(2 * pair + 1)
         first = first + pltpu.roll(first, TILE, 1)
         second = second + pltpu.roll(second, TILE, 1)
         slab[pair] = jnp.where(upper_half, second, first)
-
-    strip = BLOCKS // QUARTERS
-    for hop in range(1, QUARTERS):
-        other = lax.rem(mine + hop, QUARTERS)
-        pltpu.make_async_remote_copy(
-            src_ref=slab.at[:, pl.ds(pl.multiple_of(other * ROWS, ROWS), ROWS), :],
-            dst_ref=rows.at[pl.ds(mine * strip, strip)],
-            send_sem=send_x,
-            recv_sem=recv_x,
-            device_id=place(me - mine + other),
-            device_id_type=MESH,
-        ).start()
-    rows[pl.ds(mine * strip, strip)] = slab[:, pl.ds(pl.multiple_of(mine * ROWS, ROWS), ROWS), :]
+        for other, device in others:
+            send(slab.at[pair, row_range(other), :], rows.at[mine * strip + pair], send_x, recv_x, device)
+
+    rows[pl.ds(mine * strip, strip)] = slab[:, row_range(mine), :]
+    for k in (6, 7):
+        loads[k].wait()
     await_bytes(rows.at[pl.ds(0, BLOCKS - strip)], recv_x)
 
     waves = real_transform([rows[t] for t in range(BLOCKS)])
@@ -281,20 +294,31 @@
     def block(ref, index):
         return ref.at[pl.ds(pl.multiple_of(index * each, each), each), :]
 
-    @pl.loop(1, count)
-    def _(step):
-        to = peer(step)
-        pltpu.make_async_remote_copy(
-            src_ref=block(spectrum, to),
-            dst_ref=block(columns, me),
-            send_sem=send_b,
-            recv_sem=recv_b,
-            device_id=place(to),
-            device_id_type=MESH,
-        ).start()
+    def send_column(to_x, to_y, same_chip=False):
+        for e in range(1 if same_chip else 0, chans):
+            to_chan = chan if e == 0 else 1 - chan
+            to = (to_x * side + to_y) * chans + to_chan
+            send(block(spectrum, to), block(columns, me), send_b, recv_b, place(to_x, to_y, to_chan))
+
+    middle_way = side // 2
+    send_column(ahead(x, middle_way), ahead(y, middle_way))
+    send_column(ahead(x, middle_way), y)
+    send_column(x, ahead(y, middle_way))
+
+    @pl.loop(1, middle_way * middle_way)
+    def _(k):
+        a, b = middle_way - k // middle_way, k % middle_way
+        send_column(ahead(x, a), ahead(y, b))
+        send_column(behind(x, b), ahead(y, a))
+        send_column(behind(x, a), behind(y, b))
+        send_column(ahead(x, b), behind(y, a))
+
+    send_column(x, y, same_chip=True)
 
     own = pl.ds(pl.multiple_of(me * each, each), each)
     columns[own, :] = spectrum[own, :]
+    for k in (8, 9, 10):
+        loads[k].wait()
     await_bytes(columns.at[pl.ds(0, (count - 1) * each), :], recv_b)
 
     wide = G // ROWS
@@ -310,24 +334,27 @@
         for l2 in range(ROWS):
             out[tall * lane : tall * (lane + 1), wide * l2 : wide * (l2 + 1)] = last[tall * l2 : tall * (l2 + 1)]
 
-    await_bytes(packed.at[pl.ds(0, count - 1)], send_a)
+    await_bytes(packed.at[pl.ds(0, (line - 1) * side)], send_1)
+    await_bytes(landed.at[pl.ds(0, side - 1)], send_2)
     await_bytes(rows.at[pl.ds(0, BLOCKS - strip)], send_x)
     await_bytes(columns.at[pl.ds(0, (count - 1) * each), :], send_b)
 
 
-def body(sample_weight, fraction_u, fraction_v, cell_code, tile_fill):
+def body(*inputs):
     tiles, chans = lax.axis_size("tile"), lax.axis_size("chan")
-    count = tiles * chans
-    constants = [jnp.asarray(table) for table in tables(count)]
+    count, side = tiles * chans, math.isqrt(tiles)
+    operands = [*inputs, *(jnp.asarray(table) for table in tables(count))]
     return pl.pallas_call(
         functools.partial(kernel, tiles, chans),
         out_shape=jax.ShapeDtypeStruct((OUT_ROWS, G), F32),
-        in_specs=[pl.BlockSpec(memory_space=pltpu.VMEM)] * (5 + len(constants)),
+        in_specs=[pl.BlockSpec(memory_space=pl.ANY)] * len(operands),
         out_specs=pl.BlockSpec(memory_space=pltpu.VMEM),
-        scratch_shapes=[
+        scratch_shapes=[pltpu.VMEM(operand.shape, operand.dtype) for operand in operands]
+        + [
             pltpu.VMEM((3, NT, NT * CAP), F32),
             pltpu.VMEM((count, 3, LANES), F32),
-            pltpu.VMEM((count, 3, LANES), F32),
+            pltpu.VMEM((side, side * chans, 3, LANES), F32),
+            pltpu.VMEM((side, side * chans, 3, LANES), F32),
             pltpu.VMEM((3, LANES, count), F32),
             pltpu.VMEM((BLOCKS // QUARTERS, TILE, LANES), F32),
             pltpu.VMEM((BLOCKS, ROWS, LANES), F32),
@@ -335,10 +362,11 @@
             pltpu.VMEM((BLOCKS * ROWS, 2 * LANES), BF16),
             pltpu.VMEM((count * 8, LANES), F32),
             pltpu.VMEM((count * 8, LANES), F32),
+            pltpu.SemaphoreType.DMA((len(operands),)),
         ]
-        + [pltpu.SemaphoreType.DMA] * 6,
+        + [pltpu.SemaphoreType.DMA] * 8,
         compiler_params=pltpu.CompilerParams(collective_id=0, has_side_effects=True),
-    )(sample_weight, fraction_u, fraction_v, cell_code, tile_fill, *constants)
+    )(*operands)
 
 
 def solution(mesh):

time: 68.9 us -> 63.7 us (0.925)
  Pallas kernels: 66.8 us -> 61.7 us
    pallas_call x1, Pallas kernels: 66.8 us -> 61.7 us  [body(): pl.pallas_call(functools.partial(kernel, tiles, chans), out_shape=jax.Sha...]
where the time goes in v1:
time: 63.7 us; the launch traced here: 63.6 us
  Pallas kernels  61.7 us (97%)
  local copies, waits for them, and re-layouts  1.87 us (3%)
    pallas_call x1, Pallas kernels, body(): pl.pallas_call(functools.partial(kernel, tiles, chans), out_shape=jax.Sha...  61.7 us
    unnamed x1, local copies, waits for them, and re-layouts  1.87 us

profile of v1, /device:TPU:513, one launch (start us, length us, event | category | flops | bytes accessed | tf_op | source)
XLA Modules:
  0.0 63.6 jit_solution(11363370919218763537)
XLA Ops:
  0.0 61.7 %shard_map.109 = f32[32,4096]{1,0:T(8,128)} custom-call(f32[1,64,256]{2,1,0:T(8,128)} %refs_0_.1, f32[1,64,256]{2,1,0:T(8,128)} %refs_1_.1, f32[1,64,256]{2,1,0:T(8,128)} %refs_2_.1, s32[1,64,256]{2,1,0:T(8,128)} %refs_3_.1, s32[1,64,64]{2,1,0:T(8,128)} %refs_4_.1, bf16[64,256]{1,0:T(8,128)(2,1)} %constant.12.clone.refs_5_, ...), custom_call_target="tpu_custom_call" | custom-call | tf_op jit(solution)/shard_map/pallas_call | solution.py:347
  61.7 1.9 %copy.13 = f32[32,4096]{1,0:T(8,128)} copy(f32[32,4096]{1,0:T(8,128)} %shard_map.109) | data formatting | bytes 1048576

commit v2 on v1

--- a/solution.py
+++ b/solution.py
@@ -116,10 +116,9 @@
     load, send_1, recv_1, send_2, recv_2, send_x, recv_x, send_b, recv_b = refs[22:]
     side = math.isqrt(tiles)
     count = tiles * chans
-    line = side * chans
     layout, tile, chan = lax.axis_index("layout"), lax.axis_index("tile"), lax.axis_index("chan")
     x, y = lax.div(tile, side), lax.rem(tile, side)
-    in_line = x * chans + chan
+    along, across = jnp.where(chan == 0, x, y), jnp.where(chan == 0, y, x)
     me = tile * chans + chan
     mine = lax.rem(me, QUARTERS)
     far_first = sorted(range(side), key=lambda d: -min(d, side - d))
@@ -134,6 +133,11 @@
 
     def place(to_x, to_y, to_chan):
         return (layout, to_x * side + to_y, to_chan)
+
+    def turned_place(to_along, to_across, to_chan):
+        return place(
+            jnp.where(chan == 0, to_along, to_across), jnp.where(chan == 0, to_across, to_along), to_chan
+        )
 
     def send(src, dst, send_sem, recv_sem, device):
         pltpu.make_async_remote_copy(
@@ -148,15 +152,13 @@
     def await_bytes(ref, sem):
         pltpu.make_async_copy(ref, ref, sem).wait()
 
-    line_peers = [
-        (ahead(x, dx), chan if e == 0 else 1 - chan) for dx in far_first for e in range(chans) if (dx, e) != (0, 0)
-    ]
-    column_peers = [ahead(y, dy) for dy in far_first if dy != 0]
+    steps = [d for d in far_first if d != 0]
     barrier = pltpu.get_barrier_semaphore()
-    for to_x, to_chan in line_peers:
-        pl.semaphore_signal(barrier, inc=1, device_id=place(to_x, y, to_chan), device_id_type=MESH)
-    for to_y in column_peers:
-        pl.semaphore_signal(barrier, inc=1, device_id=place(x, to_y, chan), device_id_type=MESH)
+    senders = [turned_place(ahead(along, d), across, e) for d in steps for e in range(chans)]
+    senders += [turned_place(along, ahead(across, d), chan) for d in steps]
+    senders += [place(x, y, 1 - chan)]
+    for device in senders:
+        pl.semaphore_signal(barrier, inc=1, device_id=device, device_id_type=MESH)
 
     loads = [
         pltpu.make_async_copy(src, dst, load.at[k])
@@ -194,23 +196,31 @@
                     else:
                         row = pltpu.roll(jnp.where(lower, b, a), LANES // 2, 1)
                     to_y, to_chan = 2 * near_y + q // 2, q % 2
-                    packed[(to_x * chans + to_chan) * side + to_y, pl.ds(part, 1), :] = row
-
-    pl.semaphore_wait(barrier, len(line_peers) + len(column_peers))
-
-    for to_x, to_chan in line_peers:
-        send(
-            packed.at[pl.ds((to_x * chans + to_chan) * side, side)],
-            middle.at[:, in_line],
-            send_1,
-            recv_1,
-            place(to_x, y, to_chan),
-        )
-    middle[:, in_line] = packed[pl.ds(in_line * side, side)]
-    await_bytes(packed.at[pl.ds(0, (line - 1) * side)], recv_1)
-    for to_y in column_peers:
-        send(middle.at[to_y], landed.at[y], send_2, recv_2, place(x, to_y, chan))
-    landed[y] = middle[y]
+                    where = to_x * side + to_y if to_chan == 0 else tiles + to_y * side + to_x
+                    packed[where, pl.ds(part, 1), :] = row
+
+    pl.semaphore_wait(barrier, len(senders))
+
+    def strand(start):
+        return packed.at[pl.ds(start * side, side)]
+
+    for d in steps:
+        to_x, to_y = ahead(x, d), ahead(y, d)
+        send(strand(to_x), middle.at[:, x * chans + chan], send_1, recv_1, place(to_x, y, 0))
+        send(strand(side + to_y), middle.at[:, y * chans + chan], send_1, recv_1, place(x, to_y, 1))
+    send(
+        strand(jnp.where(chan == 0, side + y, x)),
+        middle.at[:, across * chans + chan],
+        send_1,
+        recv_1,
+        place(x, y, 1 - chan),
+    )
+    middle[:, along * chans + chan] = packed[pl.ds((chan * side + along) * side, side)]
+    await_bytes(packed.at[pl.ds(0, (2 * side - 1) * side)], recv_1)
+    for d in steps:
+        to = ahead(across, d)
+        send(middle.at[to], landed.at[across], send_2, recv_2, turned_place(along, to, chan))
+    landed[across] = middle[across]
     await_bytes(landed.at[pl.ds(0, side - 1)], recv_2)
 
     for part in range(3):
@@ -334,7 +344,7 @@
         for l2 in range(ROWS):
             out[tall * lane : tall * (lane + 1), wide * l2 : wide * (l2 + 1)] = last[tall * l2 : tall * (l2 + 1)]
 
-    await_bytes(packed.at[pl.ds(0, (line - 1) * side)], send_1)
+    await_bytes(packed.at[pl.ds(0, (2 * side - 1) * side)], send_1)
     await_bytes(landed.at[pl.ds(0, side - 1)], send_2)
     await_bytes(rows.at[pl.ds(0, BLOCKS - strip)], send_x)
     await_bytes(columns.at[pl.ds(0, (count - 1) * each), :], send_b)

time: 63.7 us -> 61.9 us (0.972)
  Pallas kernels: 61.7 us -> 59.9 us
    pallas_call x1, Pallas kernels: 61.7 us -> 59.9 us  [body(): pl.pallas_call(functools.partial(kernel, tiles, chans), out_shape=jax.Sha...]
where the time goes in v2:
time: 61.9 us; the launch traced here: 61.8 us
  Pallas kernels  59.9 us (97%)
  local copies, waits for them, and re-layouts  1.87 us (3%)
    pallas_call x1, Pallas kernels, body(): pl.pallas_call(functools.partial(kernel, tiles, chans), out_shape=jax.Sha...  59.9 us
    unnamed x1, local copies, waits for them, and re-layouts  1.87 us

profile of v2, /device:TPU:513, one launch (start us, length us, event | category | flops | bytes accessed | tf_op | source)
XLA Modules:
  0.0 61.8 jit_solution(3510915011126282287)
XLA Ops:
  0.0 59.9 %shard_map.109 = f32[32,4096]{1,0:T(8,128)} custom-call(f32[1,64,256]{2,1,0:T(8,128)} %refs_0_.1, f32[1,64,256]{2,1,0:T(8,128)} %refs_1_.1, f32[1,64,256]{2,1,0:T(8,128)} %refs_2_.1, s32[1,64,256]{2,1,0:T(8,128)} %refs_3_.1, s32[1,64,64]{2,1,0:T(8,128)} %refs_4_.1, bf16[64,256]{1,0:T(8,128)(2,1)} %constant.12.clone.refs_5_, ...), custom_call_target="tpu_custom_call" | custom-call | tf_op jit(solution)/shard_map/pallas_call | solution.py:357
  59.9 1.9 %copy.13 = f32[32,4096]{1,0:T(8,128)} copy(f32[32,4096]{1,0:T(8,128)} %shard_map.109) | data formatting | bytes 1048576

commit v3 on v2

--- a/solution.py
+++ b/solution.py
@@ -19,6 +19,7 @@
 BLOCKS = G // LANES
 OUT_ROWS = 32
 MESH = pl.DeviceIdType.MESH
+VMEM_LIMIT = 16 * 2**20
 F32 = jnp.float32
 BF16 = jnp.bfloat16
 
@@ -107,13 +108,20 @@
     return out
 
 
+def far_chips_first(side):
+    half = side // 2
+    ties = [step for j in range(side) for step in ([(half, j), (j, half)] if j != half else [(half, half)])]
+    quarter = [(a, b) for a in range(half - 1, 0, -1) for b in range(half - 1, -1, -1)]
+    quarter.sort(key=lambda step: -sum(step))
+    turned = [step for a, b in quarter for step in ((a, b), (-b, a), (-a, -b), (b, -a))]
+    return [(dx % side, dy % side) for dx, dy in ties + turned]
+
+
 def kernel(tiles, chans, *refs):
-    inputs, tables_in, refs = refs[:5], refs[5:11], refs[11:]
-    out, refs = refs[0], refs[1:]
-    weight, frac_u, frac_v, code, fill = refs[:5]
-    spread, row_table, row_twist, col_table, col_twist, last_table = refs[5:11]
-    sample, packed, middle, landed, sorted_, slab, rows, high, low, spectrum, columns = refs[11:22]
-    load, send_1, recv_1, send_2, recv_2, send_x, recv_x, send_b, recv_b = refs[22:]
+    operands, columns, refs = refs[:8], refs[8], refs[9:]
+    weight, frac_u, frac_v, code, fill, spread, row_table, row_twist = refs[:8]
+    sample, packed, middle, landed, sorted_, slab, rows, high, low, spectrum = refs[8:18]
+    load, send_1, recv_1, send_2, recv_2, send_x, recv_x, send_b, recv_b = refs[18:]
     side = math.isqrt(tiles)
     count = tiles * chans
     layout, tile, chan = lax.axis_index("layout"), lax.axis_index("tile"), lax.axis_index("chan")
@@ -124,12 +132,10 @@
     far_first = sorted(range(side), key=lambda d: -min(d, side - d))
 
     def ahead(value, step):
+        if step == 0:
+            return value
         value = value + step
         return jnp.where(value >= side, value - side, value)
-
-    def behind(value, step):
-        value = value - step
-        return jnp.where(value < 0, value + side, value)
 
     def place(to_x, to_y, to_chan):
         return (layout, to_x * side + to_y, to_chan)
@@ -162,9 +168,9 @@
 
     loads = [
         pltpu.make_async_copy(src, dst, load.at[k])
-        for k, (src, dst) in enumerate(zip([*inputs, *tables_in], refs[:11], strict=True))
+        for k, (src, dst) in enumerate(zip(operands, refs[:8], strict=True))
     ]
-    for k in (4, 5, 0, 3, 1, 2, 6, 7, 8, 9, 10):
+    for k in (4, 5, 0, 3, 1, 2, 6, 7):
         loads[k].start()
     for k in range(6):
         loads[k].wait()
@@ -310,55 +316,58 @@
             to = (to_x * side + to_y) * chans + to_chan
             send(block(spectrum, to), block(columns, me), send_b, recv_b, place(to_x, to_y, to_chan))
 
-    middle_way = side // 2
-    send_column(ahead(x, middle_way), ahead(y, middle_way))
-    send_column(ahead(x, middle_way), y)
-    send_column(x, ahead(y, middle_way))
-
-    @pl.loop(1, middle_way * middle_way)
-    def _(k):
-        a, b = middle_way - k // middle_way, k % middle_way
-        send_column(ahead(x, a), ahead(y, b))
-        send_column(behind(x, b), ahead(y, a))
-        send_column(behind(x, a), behind(y, b))
-        send_column(ahead(x, b), behind(y, a))
-
+    for dx, dy in far_chips_first(side):
+        send_column(ahead(x, dx), ahead(y, dy))
     send_column(x, y, same_chip=True)
 
-    own = pl.ds(pl.multiple_of(me * each, each), each)
-    columns[own, :] = spectrum[own, :]
-    for k in (8, 9, 10):
-        loads[k].wait()
+    own = pltpu.make_async_copy(block(spectrum, me), block(columns, me), load.at[0])
+    own.start()
+    own.wait()
     await_bytes(columns.at[pl.ds(0, (count - 1) * each), :], recv_b)
-
-    wide = G // ROWS
-    for lane in range(groups):
-        real = columns[pl.ds(lane, count, stride=each), :]
-        imag = columns[pl.ds(groups + lane, count, stride=each), :]
-        first = table_dot(col_table, jnp.concatenate([real, imag], axis=0), 0)
-        re, im = first[:wide], first[wide:]
-        c, s = col_twist[0], col_twist[1]
-        turned = jnp.concatenate([re * c - im * s, re * s + im * c], axis=1)
-        last = table_dot(last_table, turned, 1)
-        tall = LANES // ROWS
-        for l2 in range(ROWS):
-            out[tall * lane : tall * (lane + 1), wide * l2 : wide * (l2 + 1)] = last[tall * l2 : tall * (l2 + 1)]
-
     await_bytes(packed.at[pl.ds(0, (2 * side - 1) * side)], send_1)
     await_bytes(landed.at[pl.ds(0, side - 1)], send_2)
     await_bytes(rows.at[pl.ds(0, BLOCKS - strip)], send_x)
     await_bytes(columns.at[pl.ds(0, (count - 1) * each), :], send_b)
 
 
+def column_kernel(columns, col_table, col_twist, last_table, out, image, sem):
+    count = col_table.shape[1] // 2
+    each = columns.shape[0] // count
+    groups, wide, tall = each // 2, G // ROWS, LANES // ROWS
+    stores = []
+    for pair in range(0, groups, 2):
+        parts = [
+            [columns[pl.ds(part * groups + pair + extra, count, stride=each), :] for part in range(2)]
+            for extra in range(2)
+        ]
+        stacked = jnp.concatenate([jnp.concatenate(part, axis=0) for part in parts], axis=1)
+        first = table_dot(col_table, stacked, 0)
+        c, s = col_twist[0], col_twist[1]
+        for extra in range(2):
+            lane = pair + extra
+            re = first[:wide, extra * LANES : (extra + 1) * LANES]
+            im = first[wide:, extra * LANES : (extra + 1) * LANES]
+            turned = jnp.concatenate([re * c - im * s, re * s + im * c], axis=1)
+            last = table_dot(last_table, turned, 1)
+            for l2 in range(ROWS):
+                image[tall * lane : tall * (lane + 1), wide * l2 : wide * (l2 + 1)] = last[tall * l2 : tall * (l2 + 1)]
+            here = pl.ds(tall * lane, tall)
+            stores.append(pltpu.make_async_copy(image.at[here, :], out.at[here, :], sem.at[lane]))
+            stores[-1].start()
+    for store in stores:
+        store.wait()
+
+
 def body(*inputs):
     tiles, chans = lax.axis_size("tile"), lax.axis_size("chan")
     count, side = tiles * chans, math.isqrt(tiles)
-    operands = [*inputs, *(jnp.asarray(table) for table in tables(count))]
-    return pl.pallas_call(
+    constants = [jnp.asarray(table) for table in tables(count)]
+    operands = [pltpu.with_memory_space_constraint(v, pltpu.HBM) for v in [*inputs, *constants[:3]]]
+    columns = pl.pallas_call(
         functools.partial(kernel, tiles, chans),
-        out_shape=jax.ShapeDtypeStruct((OUT_ROWS, G), F32),
-        in_specs=[pl.BlockSpec(memory_space=pl.ANY)] * len(operands),
-        out_specs=pl.BlockSpec(memory_space=pltpu.VMEM),
+        out_shape=jax.ShapeDtypeStruct((count * 8, LANES), F32),
+        in_specs=[pl.BlockSpec(memory_space=pltpu.HBM)] * len(operands),
+        out_specs=pl.BlockSpec(memory_space=pl.ANY),
         scratch_shapes=[pltpu.VMEM(operand.shape, operand.dtype) for operand in operands]
         + [
             pltpu.VMEM((3, NT, NT * CAP), F32),
@@ -371,12 +380,24 @@
             pltpu.VMEM((BLOCKS * ROWS, 2 * LANES), BF16),
             pltpu.VMEM((BLOCKS * ROWS, 2 * LANES), BF16),
             pltpu.VMEM((count * 8, LANES), F32),
-            pltpu.VMEM((count * 8, LANES), F32),
             pltpu.SemaphoreType.DMA((len(operands),)),
         ]
         + [pltpu.SemaphoreType.DMA] * 8,
-        compiler_params=pltpu.CompilerParams(collective_id=0, has_side_effects=True),
+        compiler_params=pltpu.CompilerParams(
+            collective_id=0, has_side_effects=True, vmem_limit_bytes=VMEM_LIMIT
+        ),
     )(*operands)
+    return pl.pallas_call(
+        column_kernel,
+        out_shape=jax.ShapeDtypeStruct((OUT_ROWS, G), F32),
+        in_specs=[pl.BlockSpec(memory_space=pltpu.VMEM)] * 4,
+        out_specs=pl.BlockSpec(memory_space=pl.ANY),
+        scratch_shapes=[
+            pltpu.VMEM((OUT_ROWS, G), F32),
+            pltpu.SemaphoreType.DMA((BLOCKS * ROWS // LANES,)),
+        ],
+        compiler_params=pltpu.CompilerParams(vmem_limit_bytes=VMEM_LIMIT),
+    )(columns, *constants[3:])
 
 
 def solution(mesh):

time: 61.9 us -> 58.8 us (0.950)
  local copies, waits for them, and re-layouts: 1.87 us -> 0.01 us
  Pallas kernels: 59.9 us -> 58.7 us
    pallas_call x1, Pallas kernels: 59.9 us -> 56.3 us  [body(): pl.pallas_call(functools.partial(kernel, tiles, chans), out_shape=jax.Sha...]
    pallas_call x0 -> x1, Pallas kernels: none -> 2.39 us  [body(): pl.pallas_call(column_kernel, out_shape=jax.ShapeDtypeStruct((OUT_ROWS, G...]
    unnamed x1 -> x6, local copies, waits for them, and re-layouts: 1.87 us -> 0.01 us
where the time goes in v3:
time: 58.8 us; the launch traced here: 58.7 us
  Pallas kernels  58.7 us (100%)
    pallas_call x1, Pallas kernels, body(): pl.pallas_call(functools.partial(kernel, tiles, chans), out_shape=jax.Sha...  56.3 us
    pallas_call x1, Pallas kernels, body(): pl.pallas_call(column_kernel, out_shape=jax.ShapeDtypeStruct((OUT_ROWS, G...  2.39 us

profile of v3, /device:TPU:513, one launch (start us, length us, event | category | flops | bytes accessed | tf_op | source)
XLA Modules:
  0.0 58.7 jit_solution(9429654965093416842)
XLA Ops:
  0.0 0.0 copy-start
  0.0 0.0 copy-start.1
  0.0 0.0 copy-start.2
  0.0 56.3 %shard_map.109.columns = f32[1024,128]{1,0:T(8,128)S(1)} custom-call(f32[1,64,256]{2,1,0:T(8,128)} %refs_0_.1, f32[1,64,256]{2,1,0:T(8,128)} %refs_1_.1, f32[1,64,256]{2,1,0:T(8,128)} %refs_2_.1, s32[1,64,256]{2,1,0:T(8,128)} %refs_3_.1, s32[1,64,64]{2,1,0:T(8,128)} %refs_4_.1, bf16[64,256]{1,0:T(8,128)(2,1)} %constant.12.clone.refs_5_, ...), custom_call_target="tpu_custom_call" | custom-call | tf_op jit(solution)/shard_map/pallas_call | solution.py:366
  56.3 0.0 copy-done
  56.3 0.0 copy-done.1
  56.3 0.0 copy-done.2
  56.3 2.4 %shard_map.110 = f32[32,4096]{1,0:T(8,128)} custom-call(f32[1024,128]{1,0:T(8,128)S(1)} %shard_map.109.columns, bf16[1024,256]{1,0:T(8,128)(2,1)S(1)} %copy-done, f32[2,256,128]{2,1,0:T(8,128)S(1)} %copy-done.1, bf16[256,256]{1,0:T(8,128)(2,1)S(1)} %copy-done.2), custom_call_target="tpu_custom_call" | custom-call | tf_op jit(solution)/shard_map/pallas_call | solution.py:390
Async XLA Ops:
  0.0 56.3 %copy-start = (bf16[1024,256]{1,0:T(8,128)(2,1)S(1)}, bf16[1024,256]{1,0:T(8,128)(2,1)}, u32[]{:S(2)}) copy-start(bf16[1024,256]{1,0:T(8,128)(2,1)} %constant.15.clone.col_table) | copy-start | bytes 1572868
  0.0 56.3 %copy-start.1 = (f32[2,256,128]{2,1,0:T(8,128)S(1)}, f32[2,256,128]{2,1,0:T(8,128)}, u32[]{:S(2)}) copy-start(f32[2,256,128]{2,1,0:T(8,128)} %constant.16.clone.col_twist) | copy-start | bytes 786436
  0.0 56.3 %copy-start.2 = (bf16[256,256]{1,0:T(8,128)(2,1)S(1)}, bf16[256,256]{1,0:T(8,128)(2,1)}, u32[]{:S(2)}) copy-start(bf16[256,256]{1,0:T(8,128)(2,1)} %constant.17.clone.last_table) | copy-start | bytes 393220

commit v4 on v3

--- a/solution.py
+++ b/solution.py
@@ -158,6 +158,13 @@
     def await_bytes(ref, sem):
         pltpu.make_async_copy(ref, ref, sem).wait()
 
+    loads = [
+        pltpu.make_async_copy(src, dst, load.at[k])
+        for k, (src, dst) in enumerate(zip(operands, refs[:8], strict=True))
+    ]
+    for k in (4, 5, 0, 3, 1, 2, 6, 7):
+        loads[k].start()
+
     steps = [d for d in far_first if d != 0]
     barrier = pltpu.get_barrier_semaphore()
     senders = [turned_place(ahead(along, d), across, e) for d in steps for e in range(chans)]
@@ -166,12 +173,6 @@
     for device in senders:
         pl.semaphore_signal(barrier, inc=1, device_id=device, device_id_type=MESH)
 
-    loads = [
-        pltpu.make_async_copy(src, dst, load.at[k])
-        for k, (src, dst) in enumerate(zip(operands, refs[:8], strict=True))
-    ]
-    for k in (4, 5, 0, 3, 1, 2, 6, 7):
-        loads[k].start()
     for k in range(6):
         loads[k].wait()
 
@@ -265,8 +266,7 @@
     def row_range(index):
         return pl.ds(pl.multiple_of(index * ROWS, ROWS), ROWS)
 
-    @pl.loop(0, strip)
-    def _(pair):
+    for pair in range(strip):
         first, second = one_tile(2 * pair), one_tile(2 * pair + 1)
         first = first + pltpu.roll(first, TILE, 1)
         second = second + pltpu.roll(second, TILE, 1)

time: 58.8 us -> 58.5 us (level)
  no operation moved by 1% of the time
where the time goes in v4:
time: 58.5 us; the launch traced here: 58.4 us
  Pallas kernels  58.3 us (100%)
    pallas_call x1, Pallas kernels, body(): pl.pallas_call(functools.partial(kernel, tiles, chans), out_shape=jax.Sha...  55.9 us
    pallas_call x1, Pallas kernels, body(): pl.pallas_call(column_kernel, out_shape=jax.ShapeDtypeStruct((OUT_ROWS, G...  2.39 us

profile of v4, /device:TPU:513, one launch (start us, length us, event | category | flops | bytes accessed | tf_op | source)
XLA Modules:
  0.0 58.4 jit_solution(11532744787342981442)
XLA Ops:
  0.0 0.0 copy-start
  0.0 0.0 copy-start.1
  0.0 0.0 copy-start.2
  0.0 55.9 %shard_map.109.columns = f32[1024,128]{1,0:T(8,128)S(1)} custom-call(f32[1,64,256]{2,1,0:T(8,128)} %refs_0_.1, f32[1,64,256]{2,1,0:T(8,128)} %refs_1_.1, f32[1,64,256]{2,1,0:T(8,128)} %refs_2_.1, s32[1,64,256]{2,1,0:T(8,128)} %refs_3_.1, s32[1,64,64]{2,1,0:T(8,128)} %refs_4_.1, bf16[64,256]{1,0:T(8,128)(2,1)} %constant.12.clone.refs_5_, ...), custom_call_target="tpu_custom_call" | custom-call | tf_op jit(solution)/shard_map/pallas_call | solution.py:366
  56.0 0.0 copy-done
  56.0 0.0 copy-done.1
  56.0 0.0 copy-done.2
  56.0 2.4 %shard_map.110 = f32[32,4096]{1,0:T(8,128)} custom-call(f32[1024,128]{1,0:T(8,128)S(1)} %shard_map.109.columns, bf16[1024,256]{1,0:T(8,128)(2,1)S(1)} %copy-done, f32[2,256,128]{2,1,0:T(8,128)S(1)} %copy-done.1, bf16[256,256]{1,0:T(8,128)(2,1)S(1)} %copy-done.2), custom_call_target="tpu_custom_call" | custom-call | tf_op jit(solution)/shard_map/pallas_call | solution.py:390
Async XLA Ops:
  0.0 56.0 %copy-start = (bf16[1024,256]{1,0:T(8,128)(2,1)S(1)}, bf16[1024,256]{1,0:T(8,128)(2,1)}, u32[]{:S(2)}) copy-start(bf16[1024,256]{1,0:T(8,128)(2,1)} %constant.15.clone.col_table) | copy-start | bytes 1572868
  0.0 56.0 %copy-start.1 = (f32[2,256,128]{2,1,0:T(8,128)S(1)}, f32[2,256,128]{2,1,0:T(8,128)}, u32[]{:S(2)}) copy-start(f32[2,256,128]{2,1,0:T(8,128)} %constant.16.clone.col_twist) | copy-start | bytes 786436
  0.0 56.0 %copy-start.2 = (bf16[256,256]{1,0:T(8,128)(2,1)S(1)}, bf16[256,256]{1,0:T(8,128)(2,1)}, u32[]{:S(2)}) copy-start(bf16[256,256]{1,0:T(8,128)(2,1)} %constant.17.clone.last_table) | copy-start | bytes 393220

commit v5 on v4

--- a/solution.py
+++ b/solution.py
@@ -266,13 +266,23 @@
     def row_range(index):
         return pl.ds(pl.multiple_of(index * ROWS, ROWS), ROWS)
 
+    cuts = (3 * strip // 4, strip)
     for pair in range(strip):
         first, second = one_tile(2 * pair), one_tile(2 * pair + 1)
         first = first + pltpu.roll(first, TILE, 1)
         second = second + pltpu.roll(second, TILE, 1)
         slab[pair] = jnp.where(upper_half, second, first)
-        for other, device in others:
-            send(slab.at[pair, row_range(other), :], rows.at[mine * strip + pair], send_x, recv_x, device)
+        if pair + 1 in cuts:
+            first = max([0] + [cut for cut in cuts if cut <= pair])
+            some = pair + 1 - first
+            for other, device in others:
+                send(
+                    slab.at[pl.ds(first, some), row_range(other), :],
+                    rows.at[pl.ds(mine * strip + first, some)],
+                    send_x,
+                    recv_x,
+                    device,
+                )
 
     rows[pl.ds(mine * strip, strip)] = slab[:, row_range(mine), :]
     for k in (6, 7):

time: 58.5 us -> 57.2 us (0.978)
  Pallas kernels: 58.3 us -> 57 us
    pallas_call x1, Pallas kernels: 55.9 us -> 54.6 us  [body(): pl.pallas_call(functools.partial(kernel, tiles, chans), out_shape=jax.Sha...]
where the time goes in v5:
time: 57.2 us; the launch traced here: 57.1 us
  Pallas kernels  57 us (100%)
    pallas_call x1, Pallas kernels, body(): pl.pallas_call(functools.partial(kernel, tiles, chans), out_shape=jax.Sha...  54.6 us
    pallas_call x1, Pallas kernels, body(): pl.pallas_call(column_kernel, out_shape=jax.ShapeDtypeStruct((OUT_ROWS, G...  2.39 us

profile of v5, /device:TPU:513, one launch (start us, length us, event | category | flops | bytes accessed | tf_op | source)
XLA Modules:
  0.0 57.1 jit_solution(8318009151633029215)
XLA Ops:
  0.0 0.0 copy-start
  0.0 0.0 copy-start.1
  0.0 0.0 copy-start.2
  0.0 54.6 %shard_map.109.columns = f32[1024,128]{1,0:T(8,128)S(1)} custom-call(f32[1,64,256]{2,1,0:T(8,128)} %refs_0_.1, f32[1,64,256]{2,1,0:T(8,128)} %refs_1_.1, f32[1,64,256]{2,1,0:T(8,128)} %refs_2_.1, s32[1,64,256]{2,1,0:T(8,128)} %refs_3_.1, s32[1,64,64]{2,1,0:T(8,128)} %refs_4_.1, bf16[64,256]{1,0:T(8,128)(2,1)} %constant.12.clone.refs_5_, ...), custom_call_target="tpu_custom_call" | custom-call | tf_op jit(solution)/shard_map/pallas_call | solution.py:376
  54.7 0.0 copy-done
  54.7 0.0 copy-done.1
  54.7 0.0 copy-done.2
  54.7 2.4 %shard_map.110 = f32[32,4096]{1,0:T(8,128)} custom-call(f32[1024,128]{1,0:T(8,128)S(1)} %shard_map.109.columns, bf16[1024,256]{1,0:T(8,128)(2,1)S(1)} %copy-done, f32[2,256,128]{2,1,0:T(8,128)S(1)} %copy-done.1, bf16[256,256]{1,0:T(8,128)(2,1)S(1)} %copy-done.2), custom_call_target="tpu_custom_call" | custom-call | tf_op jit(solution)/shard_map/pallas_call | solution.py:400
Async XLA Ops:
  0.0 54.7 %copy-start = (bf16[1024,256]{1,0:T(8,128)(2,1)S(1)}, bf16[1024,256]{1,0:T(8,128)(2,1)}, u32[]{:S(2)}) copy-start(bf16[1024,256]{1,0:T(8,128)(2,1)} %constant.15.clone.col_table) | copy-start | bytes 1572868
  0.0 54.7 %copy-start.1 = (f32[2,256,128]{2,1,0:T(8,128)S(1)}, f32[2,256,128]{2,1,0:T(8,128)}, u32[]{:S(2)}) copy-start(f32[2,256,128]{2,1,0:T(8,128)} %constant.16.clone.col_twist) | copy-start | bytes 786436
  0.0 54.7 %copy-start.2 = (bf16[256,256]{1,0:T(8,128)(2,1)S(1)}, bf16[256,256]{1,0:T(8,128)(2,1)}, u32[]{:S(2)}) copy-start(bf16[256,256]{1,0:T(8,128)(2,1)} %constant.17.clone.last_table) | copy-start | bytes 393220

commit v6 on v5

--- a/solution.py
+++ b/solution.py
@@ -63,11 +63,9 @@
     return lax.dot_general(left, right, (((1,), (right_dim,)), ((), ())), preferred_element_type=F32)
 
 
-def table_dot(table, value, right_dim):
-    high, low = split(value)
+def table_dot(table, high, low, right_dim):
     half = table.shape[0] // 2
-    both = dot(table[...], high, right_dim)
-    return both[:half] + both[half:] + dot(table[:half], low, right_dim)
+    return dot(table[:half], high, right_dim) + dot(table[half:], high, right_dim) + dot(table[:half], low, right_dim)
 
 
 def times(value, real, imag):
@@ -258,7 +256,7 @@
     upper_half = lax.broadcasted_iota(jnp.int32, (TILE, LANES), 1) >= TILE
     strip = BLOCKS // QUARTERS
     others = []
-    for hop in range(1, QUARTERS):
+    for hop in (2, 3, 1):
         other = lax.rem(mine + hop, QUARTERS)
         index = me - mine + other
         others.append((other, (layout, lax.div(index, chans), lax.rem(index, chans))))
@@ -306,9 +304,7 @@
     groups = BLOCKS * ROWS // LANES
     for lane in range(0, groups, 2):
         where = slice(LANES * lane, LANES * (lane + 2))
-        both = dot(row_table[...], high[where], 1)
-        half = 2 * LANES
-        both = both[:half] + both[half:] + dot(row_table[:half], low[where], 1)
+        both = table_dot(row_table, high[where], low[where], 1)
         for part in range(2):
             for extra in range(2):
                 spectrum[pl.ds(part * groups + lane + extra, count, stride=2 * groups), :] = both[
@@ -351,14 +347,22 @@
             for extra in range(2)
         ]
         stacked = jnp.concatenate([jnp.concatenate(part, axis=0) for part in parts], axis=1)
-        first = table_dot(col_table, stacked, 0)
+        high, low = split(stacked)
+        tops, ends = col_table[: 2 * wide], col_table[2 * wide :]
+        real, imag = (
+            table_dot(jnp.concatenate([tops[rows], ends[rows]], axis=0), high, low, 0)
+            for rows in (slice(0, wide), slice(wide, 2 * wide))
+        )
         c, s = col_twist[0], col_twist[1]
         for extra in range(2):
             lane = pair + extra
-            re = first[:wide, extra * LANES : (extra + 1) * LANES]
-            im = first[wide:, extra * LANES : (extra + 1) * LANES]
+            re = real[:, extra * LANES : (extra + 1) * LANES]
+            im = imag[:, extra * LANES : (extra + 1) * LANES]
             turned = jnp.concatenate([re * c - im * s, re * s + im * c], axis=1)
-            last = table_dot(last_table, turned, 1)
+            high_turned, low_turned = split(turned)
+            both = dot(last_table[...], high_turned, 1)
+            half = last_table.shape[0] // 2
+            last = both[:half] + both[half:] + dot(last_table[:half], low_turned, 1)
             for l2 in range(ROWS):
                 image[tall * lane : tall * (lane + 1), wide * l2 : wide * (l2 + 1)] = last[tall * l2 : tall * (l2 + 1)]
             here = pl.ds(tall * lane, tall)

time: 57.2 us -> 56.6 us (0.990)
  Pallas kernels: 57 us -> 56.4 us
where the time goes in v6:
time: 56.6 us; the launch traced here: 56.5 us
  Pallas kernels  56.4 us (100%)
    pallas_call x1, Pallas kernels, body(): pl.pallas_call(functools.partial(kernel, tiles, chans), out_shape=jax.Sha...  54.6 us
    pallas_call x1, Pallas kernels, body(): pl.pallas_call(column_kernel, out_shape=jax.ShapeDtypeStruct((OUT_ROWS, G...  1.84 us

profile of v6, /device:TPU:513, one launch (start us, length us, event | category | flops | bytes accessed | tf_op | source)
XLA Modules:
  0.0 56.5 jit_solution(12639657303308623697)
XLA Ops:
  0.0 0.0 copy-start
  0.0 0.0 copy-start.1
  0.0 0.0 copy-start.2
  0.0 54.6 %shard_map.109.columns = f32[1024,128]{1,0:T(8,128)S(1)} custom-call(f32[1,64,256]{2,1,0:T(8,128)} %refs_0_.1, f32[1,64,256]{2,1,0:T(8,128)} %refs_1_.1, f32[1,64,256]{2,1,0:T(8,128)} %refs_2_.1, s32[1,64,256]{2,1,0:T(8,128)} %refs_3_.1, s32[1,64,64]{2,1,0:T(8,128)} %refs_4_.1, bf16[64,256]{1,0:T(8,128)(2,1)} %constant.12.clone.refs_5_, ...), custom_call_target="tpu_custom_call" | custom-call | tf_op jit(solution)/shard_map/pallas_call | solution.py:380
  54.6 0.0 copy-done
  54.6 0.0 copy-done.1
  54.6 0.0 copy-done.2
  54.6 1.8 %shard_map.110 = f32[32,4096]{1,0:T(8,128)} custom-call(f32[1024,128]{1,0:T(8,128)S(1)} %shard_map.109.columns, bf16[1024,256]{1,0:T(8,128)(2,1)S(1)} %copy-done, f32[2,256,128]{2,1,0:T(8,128)S(1)} %copy-done.1, bf16[256,256]{1,0:T(8,128)(2,1)S(1)} %copy-done.2), custom_call_target="tpu_custom_call" | custom-call | tf_op jit(solution)/shard_map/pallas_call | solution.py:404
Async XLA Ops:
  0.0 54.6 %copy-start = (bf16[1024,256]{1,0:T(8,128)(2,1)S(1)}, bf16[1024,256]{1,0:T(8,128)(2,1)}, u32[]{:S(2)}) copy-start(bf16[1024,256]{1,0:T(8,128)(2,1)} %constant.15.clone.col_table) | copy-start | bytes 1572868
  0.0 54.6 %copy-start.1 = (f32[2,256,128]{2,1,0:T(8,128)S(1)}, f32[2,256,128]{2,1,0:T(8,128)}, u32[]{:S(2)}) copy-start(f32[2,256,128]{2,1,0:T(8,128)} %constant.16.clone.col_twist) | copy-start | bytes 786436
  0.0 54.6 %copy-start.2 = (bf16[256,256]{1,0:T(8,128)(2,1)S(1)}, bf16[256,256]{1,0:T(8,128)(2,1)}, u32[]{:S(2)}) copy-start(bf16[256,256]{1,0:T(8,128)(2,1)} %constant.17.clone.last_table) | copy-start | bytes 393220

commit v7 on v6

--- a/solution.py
+++ b/solution.py
@@ -165,8 +165,10 @@
 
     steps = [d for d in far_first if d != 0]
     barrier = pltpu.get_barrier_semaphore()
-    senders = [turned_place(ahead(along, d), across, e) for d in steps for e in range(chans)]
-    senders += [turned_place(along, ahead(across, d), chan) for d in steps]
+    senders = []
+    for d in steps:
+        senders += [turned_place(ahead(along, d), across, e) for e in range(chans)]
+        senders += [turned_place(along, ahead(across, d), chan)]
     senders += [place(x, y, 1 - chan)]
     for device in senders:
         pl.semaphore_signal(barrier, inc=1, device_id=device, device_id_type=MESH)
@@ -176,13 +178,13 @@
 
     fill_wide = dot(fill[0].astype(F32).astype(BF16), spread[...], 0)
     slot = lax.broadcasted_iota(jnp.int32, (NT, NT * CAP), 1) % CAP
-    sample[0] = jnp.where(slot.astype(F32) < fill_wide, weight[0], 0.0)
+    sample[0] = jnp.where(slot.astype(F32) < fill_wide, weight[0], 0.0) * (1.0 / 65536.0)
     far = lax.broadcasted_iota(jnp.int32, (NT, NT * CAP), 0) >= NT // 2
     for part, position in (
         (1, (code[0] >> 6).astype(F32) + frac_u[0]),
         (2, (code[0] & (TILE - 1)).astype(F32) + frac_v[0]),
     ):
-        sample[part] = jnp.where(far, TILE - position, position) * 0.25
+        sample[part] = jnp.where(far, TILE - position, position)
 
     lower = lax.broadcasted_iota(jnp.int32, (1, LANES), 1) < LANES // 2
 
@@ -222,36 +224,54 @@
     )
     middle[:, along * chans + chan] = packed[pl.ds((chan * side + along) * side, side)]
     await_bytes(packed.at[pl.ds(0, (2 * side - 1) * side)], recv_1)
+    half_side = side // 2
+    own_half = lax.div(across, half_side)
     for d in steps:
         to = ahead(across, d)
-        send(middle.at[to], landed.at[across], send_2, recv_2, turned_place(along, to, chan))
+        send(middle.at[to], landed.at[across], send_2, recv_2.at[own_half], turned_place(along, to, chan))
     landed[across] = middle[across]
-    await_bytes(landed.at[pl.ds(0, side - 1)], recv_2)
-
-    for part in range(3):
-        sorted_[part] = landed[:, :, part, :].reshape(count, LANES).T
-
-    cell = lax.broadcasted_iota(jnp.int32, (TILE, count), 0).astype(F32) * 0.25
-
-    def taper(row, where):
-        scaled = cell - row[where]
-        inner = jnp.maximum(1.0 - scaled * scaled, 0.0)
+
+    cell = lax.broadcasted_iota(jnp.int32, (TILE, count), 0).astype(F32)
+    direct = lax.broadcasted_iota(jnp.int32, (1, count), 1) < count // 2
+
+    def taper(row):
+        distance = cell - row
+        inner = jnp.maximum(16.0 - distance * distance, 0.0)
         return inner * inner
 
-    def one_tile(k):
+    def one_tile(chunk, k):
+        def row_of(part, slot):
+            own = sorted_[chunk, part, pl.ds(CAP * k + slot, 1)]
+            mirrored = sorted_[chunk, part, pl.ds(NT * CAP // 2 - CAP - CAP * k + slot, 1)]
+            return jnp.where(direct, own, mirrored)
+
         total = jnp.zeros((2 * TILE, 2 * TILE), F32)
-        starts = [CAP * k, NT * CAP // 2 - CAP - CAP * k]
-        for start in starts:
-            for pair in range(CAP // 2):
-                lefts, rights = [], []
-                for slot in range(2):
-                    where = pl.ds(start + 2 * pair + slot, 1)
-                    u_high, u_low = split(taper(sorted_.at[1], where) * sorted_[0, where])
-                    v_high, v_low = split(taper(sorted_.at[2], where))
-                    lefts.append(jnp.concatenate([u_high, u_low], axis=0))
-                    rights.append(jnp.concatenate([v_high, v_low], axis=0))
-                total += dot(jnp.concatenate(lefts, axis=1), jnp.concatenate(rights, axis=1), 1)
+        for pair in range(CAP // 2):
+            lefts, rights = [], []
+            for slot in (2 * pair, 2 * pair + 1):
+                u_high, u_low = split(taper(row_of(1, slot)) * row_of(0, slot))
+                v_high, v_low = split(taper(row_of(2, slot)))
+                lefts.append(jnp.concatenate([u_high, u_low], axis=0))
+                rights.append(jnp.concatenate([v_high, v_low], axis=0))
+            total += dot(jnp.concatenate(lefts, axis=1), jnp.concatenate(rights, axis=1), 1)
         return total[:TILE] + total[TILE:]
+
+    def two_tiles(chunk, pair):
+        first, second = one_tile(chunk, 2 * pair), one_tile(chunk, 2 * pair + 1)
+        first = first + pltpu.roll(first, TILE, 1)
+        second = second + pltpu.roll(second, TILE, 1)
+        return jnp.where(upper_half, second, first)
+
+    def take_half(chunk, half):
+        for here, blocks in ((own_half == half, half_side - 1), (own_half != half, half_side)):
+
+            @pl.when(here)
+            def _():
+                await_bytes(landed.at[pl.ds(0, blocks)], recv_2.at[half])
+
+        for part in range(3):
+            some = landed[half * half_side : (half + 1) * half_side, :, part, :].reshape(count // 2, LANES)
+            sorted_[chunk, part] = jnp.concatenate([some, some], axis=0).T
 
     upper_half = lax.broadcasted_iota(jnp.int32, (TILE, LANES), 1) >= TILE
     strip = BLOCKS // QUARTERS
@@ -265,11 +285,12 @@
         return pl.ds(pl.multiple_of(index * ROWS, ROWS), ROWS)
 
     cuts = (3 * strip // 4, strip)
+    take_half(0, 1)
     for pair in range(strip):
-        first, second = one_tile(2 * pair), one_tile(2 * pair + 1)
-        first = first + pltpu.roll(first, TILE, 1)
-        second = second + pltpu.roll(second, TILE, 1)
-        slab[pair] = jnp.where(upper_half, second, first)
+        slab[pair] = two_tiles(0, pair)
+    take_half(1, 0)
+    for pair in range(strip):
+        slab[pair] += two_tiles(1, pair)
         if pair + 1 in cuts:
             first = max([0] + [cut for cut in cuts if cut <= pair])
             some = pair + 1 - first
@@ -388,7 +409,7 @@
             pltpu.VMEM((count, 3, LANES), F32),
             pltpu.VMEM((side, side * chans, 3, LANES), F32),
             pltpu.VMEM((side, side * chans, 3, LANES), F32),
-            pltpu.VMEM((3, LANES, count), F32),
+            pltpu.VMEM((2, 3, LANES, count), F32),
             pltpu.VMEM((BLOCKS // QUARTERS, TILE, LANES), F32),
             pltpu.VMEM((BLOCKS, ROWS, LANES), F32),
             pltpu.VMEM((BLOCKS * ROWS, 2 * LANES), BF16),
@@ -396,7 +417,7 @@
             pltpu.VMEM((count * 8, LANES), F32),
             pltpu.SemaphoreType.DMA((len(operands),)),
         ]
-        + [pltpu.SemaphoreType.DMA] * 8,
+        + [pltpu.SemaphoreType.DMA((2,)) if k == 3 else pltpu.SemaphoreType.DMA for k in range(8)],
         compiler_params=pltpu.CompilerParams(
             collective_id=0, has_side_effects=True, vmem_limit_bytes=VMEM_LIMIT
         ),

time: 56.6 us -> 57.4 us (1.014)
  Pallas kernels: 56.4 us -> 57.2 us
    pallas_call x1, Pallas kernels: 54.6 us -> 55.4 us  [body(): pl.pallas_call(functools.partial(kernel, tiles, chans), out_shape=jax.Sha...]
where the time goes in v7:
time: 57.4 us; the launch traced here: 57.3 us
  Pallas kernels  57.2 us (100%)
    pallas_call x1, Pallas kernels, body(): pl.pallas_call(functools.partial(kernel, tiles, chans), out_shape=jax.Sha...  55.4 us
    pallas_call x1, Pallas kernels, body(): pl.pallas_call(column_kernel, out_shape=jax.ShapeDtypeStruct((OUT_ROWS, G...  1.83 us

profile of v7, /device:TPU:513, one launch (start us, length us, event | category | flops | bytes accessed | tf_op | source)
XLA Modules:
  0.0 57.3 jit_solution(5803759843157050363)
XLA Ops:
  0.0 0.0 copy-start
  0.0 0.0 copy-start.1
  0.0 0.0 copy-start.2
  0.0 55.4 %shard_map.109.columns = f32[1024,128]{1,0:T(8,128)S(1)} custom-call(f32[1,64,256]{2,1,0:T(8,128)} %refs_0_.1, f32[1,64,256]{2,1,0:T(8,128)} %refs_1_.1, f32[1,64,256]{2,1,0:T(8,128)} %refs_2_.1, s32[1,64,256]{2,1,0:T(8,128)} %refs_3_.1, s32[1,64,64]{2,1,0:T(8,128)} %refs_4_.1, bf16[64,256]{1,0:T(8,128)(2,1)} %constant.12.clone.refs_5_, ...), custom_call_target="tpu_custom_call" | custom-call | tf_op jit(solution)/shard_map/pallas_call | solution.py:401
  55.4 0.0 copy-done
  55.4 0.0 copy-done.1
  55.4 0.0 copy-done.2
  55.5 1.8 %shard_map.110 = f32[32,4096]{1,0:T(8,128)} custom-call(f32[1024,128]{1,0:T(8,128)S(1)} %shard_map.109.columns, bf16[1024,256]{1,0:T(8,128)(2,1)S(1)} %copy-done, f32[2,256,128]{2,1,0:T(8,128)S(1)} %copy-done.1, bf16[256,256]{1,0:T(8,128)(2,1)S(1)} %copy-done.2), custom_call_target="tpu_custom_call" | custom-call | tf_op jit(solution)/shard_map/pallas_call | solution.py:425
Async XLA Ops:
  0.0 55.4 %copy-start = (bf16[1024,256]{1,0:T(8,128)(2,1)S(1)}, bf16[1024,256]{1,0:T(8,128)(2,1)}, u32[]{:S(2)}) copy-start(bf16[1024,256]{1,0:T(8,128)(2,1)} %constant.15.clone.col_table) | copy-start | bytes 1572868
  0.0 55.4 %copy-start.1 = (f32[2,256,128]{2,1,0:T(8,128)S(1)}, f32[2,256,128]{2,1,0:T(8,128)}, u32[]{:S(2)}) copy-start(f32[2,256,128]{2,1,0:T(8,128)} %constant.16.clone.col_twist) | copy-start | bytes 786436
  0.0 55.4 %copy-start.2 = (bf16[256,256]{1,0:T(8,128)(2,1)S(1)}, bf16[256,256]{1,0:T(8,128)(2,1)}, u32[]{:S(2)}) copy-start(bf16[256,256]{1,0:T(8,128)(2,1)} %constant.17.clone.last_table) | copy-start | bytes 393220

commit v8 on v6

--- a/solution.py
+++ b/solution.py
@@ -165,8 +165,10 @@
 
     steps = [d for d in far_first if d != 0]
     barrier = pltpu.get_barrier_semaphore()
-    senders = [turned_place(ahead(along, d), across, e) for d in steps for e in range(chans)]
-    senders += [turned_place(along, ahead(across, d), chan) for d in steps]
+    senders = []
+    for d in steps:
+        senders += [turned_place(ahead(along, d), across, e) for e in range(chans)]
+        senders += [turned_place(along, ahead(across, d), chan)]
     senders += [place(x, y, 1 - chan)]
     for device in senders:
         pl.semaphore_signal(barrier, inc=1, device_id=device, device_id_type=MESH)
@@ -176,13 +178,13 @@
 
     fill_wide = dot(fill[0].astype(F32).astype(BF16), spread[...], 0)
     slot = lax.broadcasted_iota(jnp.int32, (NT, NT * CAP), 1) % CAP
-    sample[0] = jnp.where(slot.astype(F32) < fill_wide, weight[0], 0.0)
+    sample[0] = jnp.where(slot.astype(F32) < fill_wide, weight[0], 0.0) * (1.0 / 65536.0)
     far = lax.broadcasted_iota(jnp.int32, (NT, NT * CAP), 0) >= NT // 2
     for part, position in (
         (1, (code[0] >> 6).astype(F32) + frac_u[0]),
         (2, (code[0] & (TILE - 1)).astype(F32) + frac_v[0]),
     ):
-        sample[part] = jnp.where(far, TILE - position, position) * 0.25
+        sample[part] = jnp.where(far, TILE - position, position)
 
     lower = lax.broadcasted_iota(jnp.int32, (1, LANES), 1) < LANES // 2
 
@@ -231,11 +233,11 @@
     for part in range(3):
         sorted_[part] = landed[:, :, part, :].reshape(count, LANES).T
 
-    cell = lax.broadcasted_iota(jnp.int32, (TILE, count), 0).astype(F32) * 0.25
+    cell = lax.broadcasted_iota(jnp.int32, (TILE, count), 0).astype(F32)
 
     def taper(row, where):
-        scaled = cell - row[where]
-        inner = jnp.maximum(1.0 - scaled * scaled, 0.0)
+        distance = cell - row[where]
+        inner = jnp.maximum(16.0 - distance * distance, 0.0)
         return inner * inner
 
     def one_tile(k):

time: 56.6 us -> 56.7 us (level)
  no operation moved by 1% of the time
where the time goes in v8:
time: 56.7 us; the launch traced here: 56.5 us
  Pallas kernels  56.5 us (100%)
    pallas_call x1, Pallas kernels, body(): pl.pallas_call(functools.partial(kernel, tiles, chans), out_shape=jax.Sha...  54.7 us
    pallas_call x1, Pallas kernels, body(): pl.pallas_call(column_kernel, out_shape=jax.ShapeDtypeStruct((OUT_ROWS, G...  1.82 us

profile of v8, /device:TPU:513, one launch (start us, length us, event | category | flops | bytes accessed | tf_op | source)
XLA Modules:
  0.0 56.5 jit_solution(14570227745143082829)
XLA Ops:
  0.0 0.0 copy-start
  0.0 0.0 copy-start.1
  0.0 0.0 copy-start.2
  0.0 54.7 %shard_map.109.columns = f32[1024,128]{1,0:T(8,128)S(1)} custom-call(f32[1,64,256]{2,1,0:T(8,128)} %refs_0_.1, f32[1,64,256]{2,1,0:T(8,128)} %refs_1_.1, f32[1,64,256]{2,1,0:T(8,128)} %refs_2_.1, s32[1,64,256]{2,1,0:T(8,128)} %refs_3_.1, s32[1,64,64]{2,1,0:T(8,128)} %refs_4_.1, bf16[64,256]{1,0:T(8,128)(2,1)} %constant.12.clone.refs_5_, ...), custom_call_target="tpu_custom_call" | custom-call | tf_op jit(solution)/shard_map/pallas_call | solution.py:382
  54.7 0.0 copy-done
  54.7 0.0 copy-done.1
  54.7 0.0 copy-done.2
  54.7 1.8 %shard_map.110 = f32[32,4096]{1,0:T(8,128)} custom-call(f32[1024,128]{1,0:T(8,128)S(1)} %shard_map.109.columns, bf16[1024,256]{1,0:T(8,128)(2,1)S(1)} %copy-done, f32[2,256,128]{2,1,0:T(8,128)S(1)} %copy-done.1, bf16[256,256]{1,0:T(8,128)(2,1)S(1)} %copy-done.2), custom_call_target="tpu_custom_call" | custom-call | tf_op jit(solution)/shard_map/pallas_call | solution.py:406
Async XLA Ops:
  0.0 54.7 %copy-start = (bf16[1024,256]{1,0:T(8,128)(2,1)S(1)}, bf16[1024,256]{1,0:T(8,128)(2,1)}, u32[]{:S(2)}) copy-start(bf16[1024,256]{1,0:T(8,128)(2,1)} %constant.15.clone.col_table) | copy-start | bytes 1572868
  0.0 54.7 %copy-start.1 = (f32[2,256,128]{2,1,0:T(8,128)S(1)}, f32[2,256,128]{2,1,0:T(8,128)}, u32[]{:S(2)}) copy-start(f32[2,256,128]{2,1,0:T(8,128)} %constant.16.clone.col_twist) | copy-start | bytes 786436
  0.0 54.7 %copy-start.2 = (bf16[256,256]{1,0:T(8,128)(2,1)S(1)}, bf16[256,256]{1,0:T(8,128)(2,1)}, u32[]{:S(2)}) copy-start(bf16[256,256]{1,0:T(8,128)(2,1)} %constant.17.clone.last_table) | copy-start | bytes 393220

commit v9 on v8

--- a/solution.py
+++ b/solution.py
@@ -165,10 +165,8 @@
 
     steps = [d for d in far_first if d != 0]
     barrier = pltpu.get_barrier_semaphore()
-    senders = []
-    for d in steps:
-        senders += [turned_place(ahead(along, d), across, e) for e in range(chans)]
-        senders += [turned_place(along, ahead(across, d), chan)]
+    senders = [turned_place(ahead(along, d), across, e) for d in steps for e in range(chans)]
+    senders += [turned_place(along, ahead(across, d), chan) for d in steps]
     senders += [place(x, y, 1 - chan)]
     for device in senders:
         pl.semaphore_signal(barrier, inc=1, device_id=device, device_id_type=MESH)

time: 56.7 us -> 56.4 us (level)
  no operation moved by 1% of the time
where the time goes in v9:
time: 56.4 us; the launch traced here: 56.3 us
  Pallas kernels  56.2 us (100%)
    pallas_call x1, Pallas kernels, body(): pl.pallas_call(functools.partial(kernel, tiles, chans), out_shape=jax.Sha...  54.4 us
    pallas_call x1, Pallas kernels, body(): pl.pallas_call(column_kernel, out_shape=jax.ShapeDtypeStruct((OUT_ROWS, G...  1.83 us

profile of v9, /device:TPU:513, one launch (start us, length us, event | category | flops | bytes accessed | tf_op | source)
XLA Modules:
  0.0 56.3 jit_solution(16895862127859633181)
XLA Ops:
  0.0 0.0 copy-start
  0.0 0.0 copy-start.1
  0.0 0.0 copy-start.2
  0.0 54.4 %shard_map.109.columns = f32[1024,128]{1,0:T(8,128)S(1)} custom-call(f32[1,64,256]{2,1,0:T(8,128)} %refs_0_.1, f32[1,64,256]{2,1,0:T(8,128)} %refs_1_.1, f32[1,64,256]{2,1,0:T(8,128)} %refs_2_.1, s32[1,64,256]{2,1,0:T(8,128)} %refs_3_.1, s32[1,64,64]{2,1,0:T(8,128)} %refs_4_.1, bf16[64,256]{1,0:T(8,128)(2,1)} %constant.12.clone.refs_5_, ...), custom_call_target="tpu_custom_call" | custom-call | tf_op jit(solution)/shard_map/pallas_call | solution.py:380
  54.4 0.0 copy-done
  54.4 0.0 copy-done.1
  54.5 0.0 copy-done.2
  54.5 1.8 %shard_map.110 = f32[32,4096]{1,0:T(8,128)} custom-call(f32[1024,128]{1,0:T(8,128)S(1)} %shard_map.109.columns, bf16[1024,256]{1,0:T(8,128)(2,1)S(1)} %copy-done, f32[2,256,128]{2,1,0:T(8,128)S(1)} %copy-done.1, bf16[256,256]{1,0:T(8,128)(2,1)S(1)} %copy-done.2), custom_call_target="tpu_custom_call" | custom-call | tf_op jit(solution)/shard_map/pallas_call | solution.py:404
Async XLA Ops:
  0.0 54.4 %copy-start = (bf16[1024,256]{1,0:T(8,128)(2,1)S(1)}, bf16[1024,256]{1,0:T(8,128)(2,1)}, u32[]{:S(2)}) copy-start(bf16[1024,256]{1,0:T(8,128)(2,1)} %constant.15.clone.col_table) | copy-start | bytes 1572868
  0.0 54.4 %copy-start.1 = (f32[2,256,128]{2,1,0:T(8,128)S(1)}, f32[2,256,128]{2,1,0:T(8,128)}, u32[]{:S(2)}) copy-start(f32[2,256,128]{2,1,0:T(8,128)} %constant.16.clone.col_twist) | copy-start | bytes 786436
  0.0 54.5 %copy-start.2 = (bf16[256,256]{1,0:T(8,128)(2,1)S(1)}, bf16[256,256]{1,0:T(8,128)(2,1)}, u32[]{:S(2)}) copy-start(bf16[256,256]{1,0:T(8,128)(2,1)} %constant.17.clone.last_table) | copy-start | bytes 393220
